TPU v7x, 32 devices: a whole 2x2x4 slice. The times are simulated.
32 devices in a mesh: dp: 32 (over z, y, x, core), mp: 1.
Axes of the slice: x: 2, y: 2, z: 4, core: 2. Of those that a mesh axis runs over, the one named last changes fastest.
Arguments:
- gradients: bfloat16 [32, 512, 6144], P('dp', None, 'mp'), may hold values from -48 to 48
- weights: bfloat16 [512, 6144], P(None, 'mp'), may hold values from -3 to 3
- master: float32 [512, 6144], P('dp', 'mp'), may hold values from -6 to 6
- moment_one: float32 [512, 6144], P('dp', 'mp'), may hold values from -6 to 6
- moment_two: float32 [512, 6144], P('dp', 'mp'), may hold values from 0.25 to 4
- group_ids: int32 [512], replicated, may hold values from 0 to 15, never falling along the last dimension, each value on 1 to 64 neighbouring positions
Outputs:
- new_weights: bfloat16 [512, 6144], P(None, 'mp')
- new_master: float32 [512, 6144], P('dp', 'mp')
- new_first: float32 [512, 6144], P('dp', 'mp')
- new_second: float32 [512, 6144], P('dp', 'mp')
Inputs may be any that keep to these rules, and one draw needn't show every extreme that they name: `group_ids`: group numbers never fall along the rows; each group has 1 to 64 rows and every group is present.
All inputs are finite; a program needn't handle non-finite values.
Results may differ from a plain program's by a relative error of at most 0.001.
The roundings to bfloat16 on the way count: a program that leaves them out, or rounds other values in their place, can miss the bound.
Values may be sent and summed in bfloat16 or wider, within the bound.
A program may use at most 64 MiB of HBM per device.

v0:
```python
import functools

import jax
import jax.numpy as jnp
from jax import lax
from jax.experimental import pallas as pl
from jax.experimental.pallas import tpu as pltpu
from jax.sharding import PartitionSpec as P

beta_one = 0.9
beta_two = 0.999
adam_eps = 1e-06
weight_decay = 0.01
learn_rate = 0.04
step_count = 100

MESH = pl.DeviceIdType.MESH
F32, BF16 = jnp.float32, jnp.bfloat16
WIDTH = 512
SKEW = 2
AG_SKEW = 2
UNROLL = 4


def flipped(bit, flag):
    return bit + flag - 2 * bit * flag


def kernel(
    n, mp, width, ids_ref, grad_ref, w_ref, master_ref, m1_ref, m2_ref,
    out_ref, new_master_ref, new_first_ref, new_second_ref,
    mine, raw, acc, recvs, held, update, member, tiles,
    mine_sem, w_sem, rs_send, rs_recv, ag_send, ag_recv, t_send, t_recv,
):
    me = lax.axis_index("dp")
    bits = [(me // 2**i) % 2 for i in range(n)]
    replicas = 2**n
    rows, cols = master_ref.shape
    chunks = cols // width
    units = [list(range(j, min(j + 2, chunks))) for j in range(0, chunks, 2)]
    orders = []
    for k in range(chunks):
        order = list(range(n))
        if n > 3:
            order[1:4] = [2, 3, 1] if k % 2 else [1, 3, 2]
        orders.append(order)

    def span(k):
        return pl.ds(k * width, width)

    def partner(flips):
        return sum(2**i * (1 - bits[i] if flips >> i & 1 else bits[i]) for i in range(n))

    low = min(n, 3)
    levels = [[{"dp": partner(f)} for f in range(1, 2**low)]]
    if n > low:
        levels.append([{"dp": partner(f << low)} for f in range(1, 2 ** (n - low))])
    if mp > 1:
        mine_mp = lax.axis_index("mp")
        places = mp.bit_length() - 1
        mp_bits = [(mine_mp // 2**i) % 2 for i in range(places)]
        levels.append([
            {"mp": sum(2**i * (1 - mp_bits[i] if f >> i & 1 else mp_bits[i]) for i in range(places))}
            for f in range(1, mp)
        ])

    w_copy = pltpu.make_async_copy(w_ref, out_ref, w_sem)
    mine_copies = [
        pltpu.make_async_copy(grad_ref.at[:, bits[0], :, span(k)], mine.at[k], mine_sem.at[k])
        for k in range(chunks)
    ]
    for copy in mine_copies:
        copy.start()

    barrier = pltpu.get_barrier_semaphore()
    greeted = [target for level in levels for target in level]
    for target in greeted:
        pl.semaphore_signal(barrier, inc=1, device_id=target, device_id_type=MESH)
    pl.semaphore_wait(barrier, len(greeted))

    started = []

    def send(src, dst, send_sem, recv_sem, target):
        copy = pltpu.make_async_remote_copy(
            src_ref=src, dst_ref=dst, send_sem=send_sem, recv_sem=recv_sem,
            device_id=target, device_id_type=MESH,
        )
        copy.start()
        started.append(copy)
        return copy

    rs = {}
    for k in range(chunks):
        rs[k, 0] = send(
            grad_ref.at[:, 1 - bits[0], :, span(k)], raw.at[k],
            rs_send.at[k, 0], rs_recv.at[k, 0], {"dp": partner(1)},
        )
    w_copy.start()

    lanes = member.shape[1]
    lane = lax.broadcasted_iota(jnp.int32, (rows, lanes), 1)
    row = lax.broadcasted_iota(jnp.int32, (rows, lanes), 0)
    own_ids = jnp.zeros((rows, lanes), jnp.int32)
    for r in range(rows):
        own_ids = jnp.where(row == r, ids_ref[me * rows + r], own_ids)
    member[...] = jnp.where(lane == own_ids, 1.0, 0.0).astype(F32)

    row_sums = {"w": jnp.zeros((rows, 1), F32), "u": jnp.zeros((rows, 1), F32)}
    correct_one = 1.0 - beta_one**step_count
    correct_two = 1.0 - beta_two**step_count

    def advance(k, s):
        order = orders[k]
        rs[k, s].wait_recv()
        if s == 0:
            mine_copies[k].wait()

            @pl.loop(0, 2 ** (n - 1), unroll=min(UNROLL, 2 ** (n - 1)))
            def _(d):
                rest = 0
                for i in range(n - 1):
                    b = order[n - 1 - i]
                    rest = rest + 2 ** (b - 1) * flipped(bits[b], (d // 2**i) % 2)
                acc[k, d] = mine[k, rest].astype(F32) + raw[k, rest].astype(F32)
            total = acc
        else:
            before = acc if s == 1 else recvs[s - 2]
            total = recvs[s - 1]

            @pl.loop(0, 2 ** (n - 1 - s), unroll=min(UNROLL, 2 ** (n - 1 - s)))
            def _(d):
                total[k, d] = total[k, d] + before[k, d]
        if s < n - 1:
            half = 2 ** (n - 2 - s)
            rs[k, s + 1] = send(
                total.at[k, pl.ds(half, half)], recvs[s].at[k],
                rs_send.at[k, s + 1], rs_recv.at[k, s + 1],
                {"dp": partner(1 << order[s + 1])},
            )
            return
        grad_mean = total[k, 0] / replicas
        master = master_ref[:, span(k)]
        new_first = beta_one * m1_ref[:, span(k)] + (1.0 - beta_one) * grad_mean
        new_second = beta_two * m2_ref[:, span(k)] + (1.0 - beta_two) * grad_mean * grad_mean
        new_first_ref[:, span(k)] = new_first
        new_second_ref[:, span(k)] = new_second
        change = (
            new_first / correct_one / (jnp.sqrt(new_second / correct_two) + adam_eps)
            + weight_decay * master
        )
        update[:, span(k)] = change
        row_sums["w"] += jnp.sum(master * master, axis=1, keepdims=True)
        row_sums["u"] += jnp.sum(change * change, axis=1, keepdims=True)

    for t in range(len(units) + SKEW * (n - 1)):
        for s in range(n):
            if 0 <= t - SKEW * s < len(units):
                for k in units[t - SKEW * s]:
                    advance(k, s)

    w_part = jnp.sum(member[...] * row_sums["w"], axis=0, keepdims=True)
    u_part = jnp.sum(member[...] * row_sums["u"], axis=0, keepdims=True)
    sub = lax.broadcasted_iota(jnp.int32, (8, lanes), 0)
    sums = jnp.where(sub == 0, w_part, u_part)
    at = 0
    for level, slots in zip(levels, tiles):
        slots[0] = sums
        copies = []
        for f, target in enumerate(level, 1):
            copies.append(send(slots.at[0], slots.at[f], t_send.at[at], t_recv.at[at], target))
            at += 1
        for f, copy in enumerate(copies, 1):
            copy.wait_recv()
            sums = sums + slots[f]
    trust = jnp.sqrt(sums[0:1] / (sums[1:2] + 1e-06))
    row_ratio = jnp.sum(member[...] * trust, axis=1, keepdims=True)
    scale = learn_rate * row_ratio

    ag = {}

    def gather(k, s):
        ag[k, s] = send(
            held.at[k, pl.ds(0, 2**s)], held.at[k, pl.ds(2**s, 2**s)],
            ag_send.at[k, s], ag_recv.at[k, s], {"dp": partner(1 << orders[k][n - 1 - s])},
        )

    for k in range(chunks):
        step = scale * update[:, span(k)]
        held[k, 0] = (-step).astype(BF16)
        gather(k, 0)
        new_master_ref[:, span(k)] = master_ref[:, span(k)] - step
    w_copy.wait()

    def apply(k, first, count):
        @pl.loop(first, first + count, unroll=min(UNROLL, count))
        def _(d):
            owner = 0
            for i in range(n):
                b = orders[k][n - 1 - i]
                owner = owner + 2**b * flipped(bits[b], (d // 2**i) % 2)
            out_ref[owner, :, span(k)] = (
                out_ref[owner, :, span(k)].astype(F32) + held[k, d].astype(F32)
            ).astype(BF16)

    for t in range(len(units) + AG_SKEW * (n - 1)):
        for s in range(n):
            if 0 <= t - AG_SKEW * s < len(units):
                for k in units[t - AG_SKEW * s]:
                    ag[k, s].wait_recv()
                    if s < n - 1:
                        gather(k, s + 1)
                    if s == n - 2:
                        apply(k, 0, 2 ** (n - 1))
                    elif s == n - 1:
                        apply(k, 2 ** (n - 1), 2 ** (n - 1))
    for copy in started:
        copy.wait_send()


def solution(mesh):
    replicas, mp = mesh.shape["dp"], mesh.shape["mp"]
    n = replicas.bit_length() - 1

    def on_device(gradients, weights, master, moment_one, moment_two, group_ids):
        rows_all, cols = weights.shape
        rows = master.shape[0]
        width = WIDTH if cols % WIDTH == 0 else 128
        chunks = cols // width
        groups = rows_all // 32
        lanes = -(-groups // 128) * 128
        low = min(n, 3)
        counts = [2**low] + ([2 ** (n - low)] if n > low else []) + ([mp] if mp > 1 else [])
        anywhere = pl.BlockSpec(memory_space=pl.ANY)
        vmem = pl.BlockSpec(memory_space=pltpu.VMEM)
        own = pltpu.VMEM((rows, cols), F32)
        dma = pltpu.SemaphoreType.DMA
        tiles_n = sum(c - 1 for c in counts)
        new_weights, new_master, new_first, new_second = pl.pallas_call(
            functools.partial(kernel, n, mp, width),
            out_shape=(pltpu.VMEM((replicas, rows, cols), BF16), own, own, own),
            in_specs=[pl.BlockSpec(memory_space=pltpu.SMEM), anywhere, anywhere, vmem, vmem, vmem],
            out_specs=(vmem, vmem, vmem, vmem),
            scratch_shapes=[
                pltpu.VMEM((chunks, replicas // 2, rows, width), BF16),
                pltpu.VMEM((chunks, replicas // 2, rows, width), BF16),
                pltpu.VMEM((chunks, replicas // 2, rows, width), F32),
                [pltpu.VMEM((chunks, 2 ** (n - 1 - s), rows, width), F32) for s in range(1, n)],
                pltpu.VMEM((chunks, replicas, rows, width), BF16),
                pltpu.VMEM((rows, cols), F32),
                pltpu.VMEM((rows, lanes), F32),
                [pltpu.VMEM((c, 8, lanes), F32) for c in counts],
                dma((chunks,)),
                dma,
                dma((chunks, n)),
                dma((chunks, n)),
                dma((chunks, n)),
                dma((chunks, n)),
                dma((tiles_n,)),
                dma((tiles_n,)),
            ],
            compiler_params=pltpu.CompilerParams(
                collective_id=0, has_side_effects=True, vmem_limit_bytes=48 * 2**20
            ),
        )(
            group_ids,
            gradients.reshape(replicas // 2, 2, rows, cols),
            weights.reshape(replicas, rows, cols),
            master, moment_one, moment_two,
        )
        return new_weights.reshape(rows_all, cols), new_master, new_first, new_second

    return jax.shard_map(
        on_device,
        mesh=mesh,
        in_specs=(P("dp", None, "mp"), P(None, "mp"), P("dp", "mp"), P("dp", "mp"), P("dp", "mp"), P()),
        out_specs=(P(None, "mp"), P("dp", "mp"), P("dp", "mp"), P("dp", "mp")),
        check_vma=False,
    )
```

profile of v0, /device:TPU:1, one launch (start us, length us, event | category | flops | bytes accessed | tf_op | source)
XLA Modules:
  0.0 114.1 jit_solution(10640639444705928325)
XLA Ops:
  0.6 108.5 %shard_map.93 = (bf16[32,16,6144]{2,1,0:T(8,128)(2,1)S(1)}, f32[16,6144]{1,0:T(8,128)S(1)}, f32[16,6144]{1,0:T(8,128)S(1)}, f32[16,6144]{1,0:T(8,128)S(1)}) custom-call(s32[512]{0:T(512)} %ids_ref.1, bf16[16,2,16,6144]{3,2,1,0:T(8,128)(2,1)} %bitcast.4, bf16[32,16,6144]{2,1,0:T(8,128)(2,1)} %bitcast.5, f32[16,6144]{1,0:T(8,128)} %master_ref.1, ...), custom_call_target="tpu_custom_call" | custom-call | tf_op jit(solution)/shard_map/pallas_call | solution.py:238
  109.2 2.7 %copy.14 = bf16[512,6144]{1,0:T(8,128)(2,1)} copy(bf16[512,6144]{1,0:T(8,128)(2,1)S(1)} %bitcast.3) | data formatting | bytes 12582912
  111.9 0.7 copy.15
  112.6 0.7 copy.16
  113.4 0.7 copy.17
where the time goes:
time: 115 us; the launch traced here: 114 us
  Pallas kernels  109 us (95%)
  local copies, waits for them, and re-layouts  4.94 us (4%)
    pallas_call x1, Pallas kernels, on_device(): pl.pallas_call(functools.partial(kernel, n, mp, width), out_shape=(pltpu....  109 us
    unnamed x4, local copies, waits for them, and re-layouts  4.94 us

commit v1 on v0

v1 whole, which is shorter than its diff:
```python
import functools

import jax
import jax.numpy as jnp
from jax import lax
from jax.experimental import pallas as pl
from jax.experimental.pallas import tpu as pltpu
from jax.sharding import PartitionSpec as P

beta_one = 0.9
beta_two = 0.999
adam_eps = 1e-06
weight_decay = 0.01
learn_rate = 0.04
step_count = 100

MESH = pl.DeviceIdType.MESH
F32, BF16, I16, I32 = jnp.float32, jnp.bfloat16, jnp.int16, jnp.int32
WIDTH = 512
LANES = 128
UNROLL = 4
TOP = 32700.0
TINY = 1e-30


def flipped(bit, flag):
    return bit + flag - 2 * bit * flag


def kernel_orders(n, chunks):
    orders = []
    for k in range(chunks):
        order = list(range(n))
        if n > 3:
            order[1:4] = [2, 3, 1] if k % 2 else [1, 3, 2]
        orders.append(order)
    return orders


def schedule(n, chunks):
    tasks = []
    for k in range(chunks):
        u = k // 2
        for s in range(n):
            tasks.append((u + 1.0 * s, -s, k, "R"))
        for s in range(n):
            tasks.append((u + 1.0 * (n + s), -(n + s), k, "A"))
    tasks.sort()
    out = []
    for _, s, k, what in tasks:
        s = -s
        out.append((what, k, s if what == "R" else s - n))
    return out


def kernel(
    n, mp, width, levels_n, ids_ref, grad_ref, w_ref, master_hbm, m1_hbm, m2_hbm,
    out_ref, new_master_ref, new_first_ref, new_second_ref,
    mine, raw, temp, kept, codes_out, codes_in, scales_out, scales_in, held, held_scale,
    update, sums, member, ratio, tiles, master_ref, m1_ref, m2_ref,
    mine_sem, w_sem, own_sem, raw_send, raw_recv, rs_send, rs_recv, rs_send2, rs_recv2,
    ag_send, ag_recv, ag_send2, ag_recv2, t_send, t_recv,
):
    me = lax.axis_index("dp")
    bits = [(me // 2**i) % 2 for i in range(n)]
    replicas = 2**n
    rows, cols = master_ref.shape
    chunks = cols // width
    lane_groups = width // LANES
    orders = kernel_orders(n, chunks)

    def span(k):
        return pl.ds(k * width, width)

    def partner(flips):
        return sum(2**i * (1 - bits[i] if flips >> i & 1 else bits[i]) for i in range(n))

    low = min(n, 3)
    levels = [[{"dp": partner(f)} for f in range(1, 2**low)]]
    if n > low:
        levels.append([{"dp": partner(f << low)} for f in range(1, 2 ** (n - low))])
    if mp > 1:
        mine_mp = lax.axis_index("mp")
        places = mp.bit_length() - 1
        mp_bits = [(mine_mp // 2**i) % 2 for i in range(places)]
        levels.append([
            {"mp": sum(2**i * (1 - mp_bits[i] if f >> i & 1 else mp_bits[i]) for i in range(places))}
            for f in range(1, mp)
        ])

    w_copy = pltpu.make_async_copy(w_ref, out_ref, w_sem)
    own_copies = [
        pltpu.make_async_copy(src, dst, own_sem.at[i])
        for i, (src, dst) in enumerate([(master_hbm, master_ref), (m1_hbm, m1_ref), (m2_hbm, m2_ref)])
    ]
    mine_copies = [
        pltpu.make_async_copy(grad_ref.at[:, bits[0], :, span(k)], mine.at[k], mine_sem.at[k])
        for k in range(chunks)
    ]
    for copy in mine_copies:
        copy.start()

    barrier = pltpu.get_barrier_semaphore()
    greeted = [target for level in levels for target in level]
    for target in greeted:
        pl.semaphore_signal(barrier, inc=1, device_id=target, device_id_type=MESH)
    pl.semaphore_wait(barrier, len(greeted))

    started = []

    def send(src, dst, send_sem, recv_sem, target):
        copy = pltpu.make_async_remote_copy(
            src_ref=src, dst_ref=dst, send_sem=send_sem, recv_sem=recv_sem,
            device_id=target, device_id_type=MESH,
        )
        copy.start()
        started.append(copy)
        return copy

    rs = {}
    for k in range(chunks):
        rs[k, 0] = [send(
            grad_ref.at[:, 1 - bits[0], :, span(k)], raw.at[k],
            raw_send.at[k], raw_recv.at[k], {"dp": partner(1)},
        )]
    for copy in own_copies:
        copy.start()
    w_copy.start()

    lane = lax.broadcasted_iota(I32, (1, LANES), 1)

    @pl.loop(0, replicas * rows, unroll=8)
    def _(r):
        member[pl.ds(r, 1), :] = jnp.where(lane == ids_ref[r], 1.0, 0.0).astype(F32)

    sums[...] = jnp.zeros_like(sums)
    correct_one = 1.0 - beta_one**step_count
    correct_two = 1.0 - beta_two**step_count

    def lanes_of(g):
        return pl.ds(g * LANES, LANES)

    def largest(values, so_far):
        for g in range(lane_groups):
            part = jnp.abs(values[:, g * LANES:(g + 1) * LANES])
            for h in range(rows // 8):
                so_far = jnp.maximum(so_far, part[h * 8:(h + 1) * 8])
        return so_far

    def scale_of(most):
        top = jnp.maximum(jnp.max(most, axis=0, keepdims=True), TINY)
        return top * (1.0 / TOP), TOP / top

    def code(value):
        return jnp.round(value).astype(I32).astype(I16)

    def wide(row):
        return jnp.concatenate([row] * lane_groups, axis=1)

    def rest_of(order, d):
        rest = 0
        for i in range(n - 1):
            b = order[n - 1 - i]
            rest = rest + 2 ** (b - 1) * flipped(bits[b], (d // 2**i) % 2)
        return rest

    def reduce(k, s):
        order = orders[k]
        for copy in rs[k, s]:
            copy.wait_recv()
        if s == 0:
            mine_copies[k].wait()

        if s:
            scale_in = wide(scales_in[s - 1][k])

        def total(d):
            if s == 0:
                rest = rest_of(order, d)
                return mine[k, rest].astype(F32) + raw[k, rest].astype(F32)
            got = codes_in[s - 1][k, d].astype(F32) * scale_in
            if s == 1:
                rest = rest_of(order, d)
                return mine[k, rest].astype(F32) + raw[k, rest].astype(F32) + got
            return kept[k, d] + got

        if s < n - 1:
            half = 2 ** (n - 2 - s)

            @pl.loop(0, half, init_carry=jnp.zeros((8, LANES), F32), unroll=min(UNROLL, half))
            def most(d, so_far):
                value = total(half + d)
                temp[d] = value
                return largest(value, so_far)

            scale, inverse = scale_of(most)
            scales_out[s][k] = scale
            spread = wide(inverse)

            @pl.loop(0, half, unroll=min(UNROLL, half))
            def _(d):
                codes_out[s][k, d] = code(temp[d] * spread)

            target = {"dp": partner(1 << order[s + 1])}
            rs[k, s + 1] = [
                send(codes_out[s].at[k], codes_in[s].at[k], rs_send.at[k, s], rs_recv.at[k, s], target),
                send(scales_out[s].at[k], scales_in[s].at[k], rs_send2.at[k, s], rs_recv2.at[k, s], target),
            ]
            if s:

                @pl.loop(0, half, unroll=min(UNROLL, half))
                def _(d):
                    kept[k, d] = total(d)
            return
        if k == first_done:
            for copy in own_copies:
                copy.wait()
        grad_mean = total(0) / replicas
        master = master_ref[:, span(k)]
        new_first = beta_one * m1_ref[:, span(k)] + (1.0 - beta_one) * grad_mean
        new_second = beta_two * m2_ref[:, span(k)] + (1.0 - beta_two) * grad_mean * grad_mean
        change = (
            new_first / correct_one / (jnp.sqrt(new_second / correct_two) + adam_eps)
            + weight_decay * master
        )
        scale, inverse = scale_of(largest(change, jnp.zeros((8, LANES), F32)))
        held_scale[k, 0] = scale
        held[k, 0] = code(change * wide(inverse))
        gather(k, 0)
        update[:, span(k)] = change
        new_first_ref[:, span(k)] = new_first
        new_second_ref[:, span(k)] = new_second
        for i, value in enumerate((master, change)):
            square = value * value
            sums[i] += sum(square[:, g * LANES:(g + 1) * LANES] for g in range(lane_groups))

    ag = {}

    def gather(k, s):
        target = {"dp": partner(1 << orders[k][n - 1 - s])}
        here, there = pl.ds(0, 2**s), pl.ds(2**s, 2**s)
        ag[k, s] = [
            send(held.at[k, here], held.at[k, there], ag_send.at[k, s], ag_recv.at[k, s], target),
            send(held_scale.at[k, here], held_scale.at[k, there], ag_send2.at[k, s], ag_recv2.at[k, s], target),
        ]

    def expand(k, s):
        for copy in ag[k, s]:
            copy.wait_recv()
        if s < n - 1:
            gather(k, s + 1)

    trust_state = {}
    trust_at = [0]

    def trust_send(level):
        slots = tiles[level]
        slots[0] = trust_state["sums"]
        copies = []
        for f, target in enumerate(levels[level], 1):
            at = trust_at[0]
            copies.append(send(slots.at[0], slots.at[f], t_send.at[at], t_recv.at[at], target))
            trust_at[0] += 1
        trust_state["copies"] = copies

    def trust_start():
        own = member[pl.ds(pl.multiple_of(me * rows, rows), rows), :]
        w_part = jnp.sum(own * jnp.sum(sums[0], axis=1, keepdims=True), axis=0, keepdims=True)
        u_part = jnp.sum(own * jnp.sum(sums[1], axis=1, keepdims=True), axis=0, keepdims=True)
        sub = lax.broadcasted_iota(I32, (8, LANES), 0)
        trust_state["sums"] = jnp.where(sub == 0, w_part, u_part)
        trust_send(0)

    def trust_next(level):
        total = trust_state["sums"]
        for f, copy in enumerate(trust_state["copies"], 1):
            copy.wait_recv()
            total = total + tiles[level][f]
        trust_state["sums"] = total
        if level + 1 < len(levels):
            trust_send(level + 1)
            return
        trust = jnp.sqrt(total[0:1] / (total[1:2] + 1e-06))

        @pl.loop(0, replicas, unroll=4)
        def _(d):
            at = pl.ds(pl.multiple_of(d * rows, rows), rows)
            row_ratio = jnp.sum(member[at, :] * trust, axis=1, keepdims=True)
            ratio[at, :] = jnp.broadcast_to(-learn_rate * row_ratio, (rows, LANES))

    def own_master():
        at = pl.ds(pl.multiple_of(me * rows, rows), rows)
        down = ratio[at, :]
        for g in range(cols // LANES):
            new_master_ref[:, lanes_of(g)] = master_ref[:, lanes_of(g)] + down * update[:, lanes_of(g)]

    def apply(k):
        @pl.loop(0, replicas, unroll=min(UNROLL, replicas))
        def _(d):
            owner = 0
            for i in range(n):
                b = orders[k][n - 1 - i]
                owner = owner + 2**b * flipped(bits[b], (d // 2**i) % 2)
            at = pl.ds(pl.multiple_of(owner * rows, rows), rows)
            factor = ratio[at, :] * held_scale[k, d]
            delta = (held[k, d].astype(F32) * wide(factor)).astype(BF16)
            out_ref[owner, :, span(k)] = (
                out_ref[owner, :, span(k)].astype(F32) + delta.astype(F32)
            ).astype(BF16)

    order = schedule(n, chunks)
    ends = [i for i, task in enumerate(order) if task[0] == "R" and task[2] == n - 1]
    first_done = order[ends[0]][1]
    last_update = ends[-1]
    applied, gathered, trusted, since = set(), [], -1, 0
    for i, (what, k, s) in enumerate(order):
        if what == "R":
            reduce(k, s)
        else:
            expand(k, s)
            if s == n - 1:
                gathered.append(k)
        if i == last_update:
            trust_start()
            trusted, since = 0, 0
        elif 0 <= trusted < len(levels):
            since += 1
            if since == 2:
                trust_next(trusted)
                trusted, since = trusted + 1, 0
                if trusted == len(levels):
                    own_master()
                    w_copy.wait()
        elif trusted == len(levels):
            for j in [j for j in gathered if j not in applied][:2]:
                apply(j)
                applied.add(j)
    while trusted < len(levels):
        trust_next(trusted)
        trusted += 1
        if trusted == len(levels):
            own_master()
            w_copy.wait()
    for j in gathered:
        if j not in applied:
            apply(j)
    for copy in started:
        copy.wait_send()


def solution(mesh):
    replicas, mp = mesh.shape["dp"], mesh.shape["mp"]
    n = replicas.bit_length() - 1

    def on_device(gradients, weights, master, moment_one, moment_two, group_ids):
        rows_all, cols = weights.shape
        rows = master.shape[0]
        width = WIDTH if cols % WIDTH == 0 else LANES
        chunks = cols // width
        low = min(n, 3)
        counts = [2**low] + ([2 ** (n - low)] if n > low else []) + ([mp] if mp > 1 else [])
        anywhere = pl.BlockSpec(memory_space=pl.ANY)
        vmem = pl.BlockSpec(memory_space=pltpu.VMEM)
        own = pltpu.VMEM((rows, cols), F32)
        dma = pltpu.SemaphoreType.DMA
        tiles_n = sum(c - 1 for c in counts)
        halves = [2 ** (n - 2 - s) for s in range(n - 1)]
        codes = [pltpu.VMEM((chunks, half, rows, width), I16) for half in halves]
        scales = [pltpu.VMEM((chunks, 1, LANES), F32) for _ in halves]
        new_weights, new_master, new_first, new_second = pl.pallas_call(
            functools.partial(kernel, n, mp, width, len(counts)),
            out_shape=(pltpu.VMEM((replicas, rows, cols), BF16), own, own, own),
            in_specs=[pl.BlockSpec(memory_space=pltpu.SMEM)] + [anywhere] * 5,
            out_specs=(vmem, vmem, vmem, vmem),
            scratch_shapes=[
                pltpu.VMEM((chunks, replicas // 2, rows, width), BF16),
                pltpu.VMEM((chunks, replicas // 2, rows, width), BF16),
                pltpu.VMEM((replicas // 4, rows, width), F32),
                pltpu.VMEM((chunks, max(replicas // 8, 1), rows, width), F32),
                codes, codes, scales, scales,
                pltpu.VMEM((chunks, replicas, rows, width), I16),
                pltpu.VMEM((chunks, replicas, 1, LANES), F32),
                pltpu.VMEM((rows, cols), F32),
                pltpu.VMEM((2, rows, LANES), F32),
                pltpu.VMEM((rows_all, LANES), F32),
                pltpu.VMEM((rows_all, LANES), F32),
                [pltpu.VMEM((c, 8, LANES), F32) for c in counts],
                own, own, own,
                dma((chunks,)), dma, dma((3,)),
                dma((chunks,)), dma((chunks,)),
                dma((chunks, n - 1)), dma((chunks, n - 1)), dma((chunks, n - 1)), dma((chunks, n - 1)),
                dma((chunks, n)), dma((chunks, n)), dma((chunks, n)), dma((chunks, n)),
                dma((tiles_n,)), dma((tiles_n,)),
            ],
            compiler_params=pltpu.CompilerParams(
                collective_id=0, has_side_effects=True, vmem_limit_bytes=52 * 2**20
            ),
        )(
            group_ids,
            gradients.reshape(replicas // 2, 2, rows, cols),
            weights.reshape(replicas, rows, cols),
            master, moment_one, moment_two,
        )
        return new_weights.reshape(rows_all, cols), new_master, new_first, new_second

    return jax.shard_map(
        on_device,
        mesh=mesh,
        in_specs=(P("dp", None, "mp"), P(None, "mp"), P("dp", "mp"), P("dp", "mp"), P("dp", "mp"), P()),
        out_specs=(P(None, "mp"), P("dp", "mp"), P("dp", "mp"), P("dp", "mp")),
        check_vma=False,
    )
```

time: 115 us -> 94.1 us (0.82)
  Pallas kernels: 109 us -> 88.3 us
    pallas_call x1, Pallas kernels: 109 us -> 88.3 us  [on_device(): pl.pallas_call(functools.partial(kernel, n, mp, width, len(counts)), out_...]
where the time goes in v1:
time: 94.1 us; the launch traced here: 93.9 us
  Pallas kernels  88.3 us (94%)
  local copies, waits for them, and re-layouts  4.94 us (5%)
    pallas_call x1, Pallas kernels, on_device(): pl.pallas_call(functools.partial(kernel, n, mp, width, len(counts)), out_...  88.3 us
    unnamed x4, local copies, waits for them, and re-layouts  4.94 us

profile of v1, /device:TPU:1, one launch (start us, length us, event | category | flops | bytes accessed | tf_op | source)
XLA Modules:
  0.0 93.9 jit_solution(9567191018697282266)
XLA Ops:
  0.6 88.3 %shard_map.93 = (bf16[32,16,6144]{2,1,0:T(8,128)(2,1)S(1)}, f32[16,6144]{1,0:T(8,128)S(1)}, f32[16,6144]{1,0:T(8,128)S(1)}, f32[16,6144]{1,0:T(8,128)S(1)}) custom-call(s32[512]{0:T(512)} %ids_ref.1, bf16[16,2,16,6144]{3,2,1,0:T(8,128)(2,1)} %bitcast.4, bf16[32,16,6144]{2,1,0:T(8,128)(2,1)} %bitcast.5, f32[16,6144]{1,0:T(8,128)} %master_hbm.1, ...), custom_call_target="tpu_custom_call" | custom-call | tf_op jit(solution)/shard_map/pallas_call | solution.py:370
  88.9 2.7 %copy.14 = bf16[512,6144]{1,0:T(8,128)(2,1)} copy(bf16[512,6144]{1,0:T(8,128)(2,1)S(1)} %bitcast.3) | data formatting | bytes 12582912
  91.6 0.7 copy.15
  92.4 0.7 copy.16
  93.1 0.7 copy.17

commit v2 on v1

v2 whole, which is shorter than its diff:
```python
import functools

import jax
import jax.numpy as jnp
from jax import lax
from jax.experimental import pallas as pl
from jax.experimental.pallas import tpu as pltpu
from jax.sharding import PartitionSpec as P

beta_one = 0.9
beta_two = 0.999
adam_eps = 1e-06
weight_decay = 0.01
learn_rate = 0.04
step_count = 100

MESH = pl.DeviceIdType.MESH
F32, BF16, I16, I32 = jnp.float32, jnp.bfloat16, jnp.int16, jnp.int32
WIDTH = 512
LANES = 128
STATIC = 8
SKEW = 2
TOP = 32700.0
TINY = 1e-30


def flipped(bit, flag):
    if isinstance(flag, int):
        return 1 - bit if flag else bit
    return bit + flag - 2 * bit * flag


def over_slots(first, count, step):
    fixed = min(count, STATIC)
    places = count.bit_length() - 1
    low = fixed.bit_length() - 1

    def run(high):
        if len(high) < places - low:

            @pl.loop(0, 2)
            def _(bit):
                run([bit] + high)
            return
        for i in range(fixed):
            step([i >> p & 1 for p in range(low)] + high + ([1] if first else []))

    run([])


def slot(flags):
    return sum(2**p * flag for p, flag in enumerate(flags))


def kernel_orders(n, chunks):
    orders = []
    for k in range(chunks):
        order = list(range(n))
        if n > 3:
            order[1:4] = [2, 3, 1] if k % 2 else [1, 3, 2]
        orders.append(order)
    return orders


def schedule(n, chunks, levels):
    tasks = []
    for k in range(chunks):
        u = k // 2
        for s in range(2 * n):
            what = ("R", k, s) if s < n else ("A", k, s - n)
            tasks.append((u + SKEW * s, 2 * n - s, k, what))
    tasks.sort()
    order = [what for *_, what in tasks]
    last = max(i for i, task in enumerate(order) if task[0] == "R")
    out, ready, level, since = [], [], 0, 0
    for i, task in enumerate(order):
        out.append(task)
        if task[0] == "A" and task[2] == n - 1:
            ready.append(task[1])
        if i == last:
            out.append(("T", 0, 0))
            level, since = 1, 0
        elif 0 < level <= levels:
            since += 1
            if since == 2:
                out.append(("T", 0, level))
                level, since = level + 1, 0
        elif level > levels:
            for k in ready[:2]:
                out.append(("P", k, 0))
            ready = ready[2:]
    while level <= levels:
        out.append(("T", 0, level))
        level += 1
    return out + [("P", k, 0) for k in ready]


def kernel(
    n, mp, width, levels_n, ids_ref, grad_ref, w_ref, master_hbm, m1_hbm, m2_hbm,
    out_ref, new_master_ref, new_first_ref, new_second_ref,
    mine, raw, temp, peak, kept, codes_out, codes_in, scales_out, scales_in, held, held_scale,
    update, sums, member, ratio, tiles, state, units,
    mine_sem, w_sem, own_sem, raw_send, raw_recv, rs_send, rs_recv, ag_send, ag_recv, t_send, t_recv,
):
    me = lax.axis_index("dp")
    bits = [(me // 2**i) % 2 for i in range(n)]
    replicas = 2**n
    _, rows, cols = state.shape
    master_ref, m1_ref, m2_ref = (state.at[i] for i in range(3))
    chunks = cols // width
    lane_groups = width // LANES
    orders = kernel_orders(n, chunks)

    def span(k):
        return pl.ds(k * width, width)

    def partner(flips):
        return sum(2**i * (1 - bits[i] if flips >> i & 1 else bits[i]) for i in range(n))

    low = min(n, 3)
    levels = [[{"dp": partner(f)} for f in range(1, 2**low)]]
    if n > low:
        levels.append([{"dp": partner(f << low)} for f in range(1, 2 ** (n - low))])
    if mp > 1:
        mine_mp = lax.axis_index("mp")
        places = mp.bit_length() - 1
        mp_bits = [(mine_mp // 2**i) % 2 for i in range(places)]
        levels.append([
            {"mp": sum(2**i * (1 - mp_bits[i] if f >> i & 1 else mp_bits[i]) for i in range(places))}
            for f in range(1, mp)
        ])

    w_copy = pltpu.make_async_copy(w_ref, out_ref, w_sem)
    own_copies = [
        pltpu.make_async_copy(src, state.at[i], own_sem) for i, src in enumerate([master_hbm, m1_hbm, m2_hbm])
    ]
    mine_copies = [
        pltpu.make_async_copy(grad_ref.at[:, bits[0], :, span(k)], mine.at[k], mine_sem)
        for k in range(chunks)
    ]
    for copy in mine_copies:
        copy.start()

    barrier = pltpu.get_barrier_semaphore()
    greeted = [target for level in levels for target in level]
    for target in greeted:
        pl.semaphore_signal(barrier, inc=1, device_id=target, device_id_type=MESH)
    pl.semaphore_wait(barrier, len(greeted))

    def finish(ref, sem):
        pltpu.make_async_copy(ref, ref, sem).wait()

    def finish_coded(slots, scales, sem):
        row = LANES * 4
        count = (slots * rows * width * 2 + scales * row) // row
        finish(units.at[pl.ds(0, count)], sem)

    def send(src, dst, send_sem, recv_sem, target):
        copy = pltpu.make_async_remote_copy(
            src_ref=src, dst_ref=dst, send_sem=send_sem, recv_sem=recv_sem,
            device_id=target, device_id_type=MESH,
        )
        copy.start()

    for k in range(chunks):
        send(
            grad_ref.at[:, 1 - bits[0], :, span(k)], raw.at[k], raw_send, raw_recv.at[k], {"dp": partner(1)}
        )
    for copy in own_copies:
        copy.start()
    w_copy.start()

    lane = lax.broadcasted_iota(I32, (1, LANES), 1)

    @pl.loop(0, replicas * rows, unroll=8)
    def _(r):
        member[pl.ds(r, 1), :] = jnp.where(lane == ids_ref[r], 1.0, 0.0).astype(F32)

    sums[...] = jnp.zeros_like(sums)
    correct_one = 1.0 - beta_one**step_count
    correct_two = 1.0 - beta_two**step_count

    def lanes_of(g):
        return pl.ds(g * LANES, LANES)

    def largest(values, so_far):
        for g in range(lane_groups):
            part = jnp.abs(values[:, g * LANES:(g + 1) * LANES])
            for h in range(rows // 8):
                so_far = jnp.maximum(so_far, part[h * 8:(h + 1) * 8])
        return so_far

    def scale_of(most):
        top = jnp.maximum(jnp.max(most, axis=0, keepdims=True), TINY)
        return top * (1.0 / TOP), TOP / top

    def code(value):
        return jnp.round(value).astype(I32).astype(I16)

    def wide(row):
        return jnp.concatenate([row] * lane_groups, axis=1)

    def label_of(order, flags):
        label = [None] * n
        for i, flag in enumerate(flags):
            label[order[n - 1 - i]] = flipped(bits[order[n - 1 - i]], flag)
        for b in range(n):
            if label[b] is None:
                label[b] = bits[b]
        return label

    def both(k, flags):
        rest = sum(2 ** (b - 1) * bit for b, bit in enumerate(label_of(orders[k], flags)) if b)
        return mine[k, rest].astype(F32) + raw[k, rest].astype(F32)

    def reduce(k, s):
        order = orders[k]
        if s == 0:
            if k == first_taken:
                finish(mine, mine_sem)
            finish(raw.at[k], raw_recv.at[k])
        else:
            finish_coded(2 ** (n - 1 - s), 1, rs_recv.at[k, s - 1])
            scale_in = wide(scales_in[s - 1][k])

        def total(flags):
            if s == 0:
                return both(k, flags)
            d = slot(flags)
            got = codes_in[s - 1][k, d].astype(F32) * scale_in
            return (both(k, flags) if s == 1 else kept[k, d]) + got

        if s < n - 1:
            half = 2 ** (n - 2 - s)
            peak[...] = jnp.zeros_like(peak)

            def add(flags):
                value = total(flags)
                temp[slot(flags[:-1])] = value
                peak[...] = largest(value, peak[...])

            over_slots(half, half, add)
            scale, inverse = scale_of(peak[...])
            scales_out[s][k] = scale
            spread = wide(inverse)

            def encode(flags):
                d = slot(flags)
                codes_out[s][k, d] = code(temp[d] * spread)

            over_slots(0, half, encode)
            target = {"dp": partner(1 << order[s + 1])}
            send(codes_out[s].at[k], codes_in[s].at[k], rs_send.at[s, 0], rs_recv.at[k, s], target)
            send(scales_out[s].at[k], scales_in[s].at[k], rs_send.at[s, 1], rs_recv.at[k, s], target)
            if s:

                def keep(flags):
                    kept[k, slot(flags)] = total(flags)

                over_slots(0, half, keep)
            return
        if k == first_done:
            finish(state, own_sem)
        grad_mean = total([]) / replicas
        master = master_ref[:, span(k)]
        new_first = beta_one * m1_ref[:, span(k)] + (1.0 - beta_one) * grad_mean
        new_second = beta_two * m2_ref[:, span(k)] + (1.0 - beta_two) * grad_mean * grad_mean
        change = (
            new_first / correct_one / (jnp.sqrt(new_second / correct_two) + adam_eps)
            + weight_decay * master
        )
        scale, inverse = scale_of(largest(change, jnp.zeros((8, LANES), F32)))
        held_scale[k, 0] = scale
        held[k, 0] = code(change * wide(inverse))
        pass_on(k, -1)
        update[:, span(k)] = change
        new_first_ref[:, span(k)] = new_first
        new_second_ref[:, span(k)] = new_second
        for i, value in enumerate((master, change)):
            square = value * value
            sums[i] += sum(square[:, g * LANES:(g + 1) * LANES] for g in range(lane_groups))

    def gather(k, s, piece):
        target = {"dp": partner(1 << orders[k][n - 1 - s])}
        count = max(2 ** (s - 1), 1)
        first = count if s and piece else 0
        here, there = pl.ds(first, count), pl.ds(first + 2**s, count)
        send(held.at[k, here], held.at[k, there], ag_send.at[s, 0], ag_recv.at[k, s], target)
        send(held_scale.at[k, here], held_scale.at[k, there], ag_send.at[s, 1], ag_recv.at[k, s], target)

    def pass_on(k, s):
        if s + 1 < n:
            gather(k, s + 1, 1)
        if s + 2 < n:
            gather(k, s + 2, 0)

    def expand(k, s):
        finish_coded(2**s, 2**s, ag_recv.at[k, s])
        pass_on(k, s)

    trust_state = {}

    def trust_send(level):
        slots = tiles[level]
        slots[0] = trust_state["sums"]
        for f, target in enumerate(levels[level], 1):
            send(slots.at[0], slots.at[f], t_send.at[level], t_recv.at[level], target)

    def trust_start():
        own = member[pl.ds(pl.multiple_of(me * rows, rows), rows), :]
        w_part = jnp.sum(own * jnp.sum(sums[0], axis=1, keepdims=True), axis=0, keepdims=True)
        u_part = jnp.sum(own * jnp.sum(sums[1], axis=1, keepdims=True), axis=0, keepdims=True)
        sub = lax.broadcasted_iota(I32, (8, LANES), 0)
        trust_state["sums"] = jnp.where(sub == 0, w_part, u_part)
        trust_send(0)

    def trust_next(level):
        total = trust_state["sums"]
        others = len(levels[level])
        finish(tiles[level].at[pl.ds(1, others)], t_recv.at[level])
        for f in range(1, others + 1):
            total = total + tiles[level][f]
        trust_state["sums"] = total
        if level + 1 < len(levels):
            trust_send(level + 1)
            return
        trust = jnp.sqrt(total[0:1] / (total[1:2] + 1e-06))

        @pl.loop(0, replicas, unroll=4)
        def _(d):
            at = pl.ds(pl.multiple_of(d * rows, rows), rows)
            row_ratio = jnp.sum(member[at, :] * trust, axis=1, keepdims=True)
            ratio[at, :] = jnp.broadcast_to(-learn_rate * row_ratio, (rows, LANES))

    def own_master():
        at = pl.ds(pl.multiple_of(me * rows, rows), rows)
        down = ratio[at, :]
        for g in range(cols // LANES):
            new_master_ref[:, lanes_of(g)] = master_ref[:, lanes_of(g)] + down * update[:, lanes_of(g)]

    def apply(k):
        def one(flags):
            d = slot(flags)
            owner = sum(2**b * bit for b, bit in enumerate(label_of(orders[k], flags)))
            at = pl.ds(pl.multiple_of(owner * rows, rows), rows)
            factor = ratio[at, :] * held_scale[k, d]
            delta = (held[k, d].astype(F32) * wide(factor)).astype(BF16)
            out_ref[owner, :, span(k)] = (
                out_ref[owner, :, span(k)].astype(F32) + delta.astype(F32)
            ).astype(BF16)

        over_slots(0, replicas, one)

    order = schedule(n, chunks, len(levels))
    first_taken = order[0][1]
    first_done = next(k for what, k, s in order if what == "R" and s == n - 1)
    for what, k, s in order:
        if what == "R":
            reduce(k, s)
        elif what == "A":
            expand(k, s)
        elif what == "P":
            apply(k)
        elif s == 0:
            trust_start()
        else:
            trust_next(s - 1)
            if s == len(levels):
                own_master()
                w_copy.wait()
    finish(raw, raw_send)
    for s in range(n - 1):
        finish(codes_out[s], rs_send.at[s, 0])
        finish(scales_out[s], rs_send.at[s, 1])
    for s in range(n):
        finish(held.at[:, pl.ds(0, 2**s)], ag_send.at[s, 0])
        finish(held_scale.at[:, pl.ds(0, 2**s)], ag_send.at[s, 1])
    for i, slots in enumerate(tiles):
        finish(slots.at[pl.ds(1, len(levels[i]))], t_send.at[i])


def solution(mesh):
    replicas, mp = mesh.shape["dp"], mesh.shape["mp"]
    n = replicas.bit_length() - 1

    def on_device(gradients, weights, master, moment_one, moment_two, group_ids):
        rows_all, cols = weights.shape
        rows = master.shape[0]
        width = WIDTH if cols % WIDTH == 0 else LANES
        chunks = cols // width
        low = min(n, 3)
        counts = [2**low] + ([2 ** (n - low)] if n > low else []) + ([mp] if mp > 1 else [])
        anywhere = pl.BlockSpec(memory_space=pl.ANY)
        vmem = pl.BlockSpec(memory_space=pltpu.VMEM)
        own = pltpu.VMEM((rows, cols), F32)
        dma = pltpu.SemaphoreType.DMA
        halves = [2 ** (n - 2 - s) for s in range(n - 1)]
        codes = [pltpu.VMEM((chunks, half, rows, width), I16) for half in halves]
        scales = [pltpu.VMEM((chunks, 1, LANES), F32) for _ in halves]
        new_weights, new_master, new_first, new_second = pl.pallas_call(
            functools.partial(kernel, n, mp, width, len(counts)),
            out_shape=(pltpu.VMEM((replicas, rows, cols), BF16), own, own, own),
            in_specs=[pl.BlockSpec(memory_space=pltpu.SMEM)] + [anywhere] * 5,
            out_specs=(vmem, vmem, vmem, vmem),
            scratch_shapes=[
                pltpu.VMEM((chunks, replicas // 2, rows, width), BF16),
                pltpu.VMEM((chunks, replicas // 2, rows, width), BF16),
                pltpu.VMEM((replicas // 4, rows, width), F32),
                pltpu.VMEM((8, LANES), F32),
                pltpu.VMEM((chunks, max(replicas // 8, 1), rows, width), F32),
                codes, codes, scales, scales,
                pltpu.VMEM((chunks, replicas, rows, width), I16),
                pltpu.VMEM((chunks, replicas, 1, LANES), F32),
                pltpu.VMEM((rows, cols), F32),
                pltpu.VMEM((2, rows, LANES), F32),
                pltpu.VMEM((rows_all, LANES), F32),
                pltpu.VMEM((rows_all, LANES), F32),
                [pltpu.VMEM((c, 8, LANES), F32) for c in counts],
                pltpu.VMEM((3, rows, cols), F32),
                pltpu.VMEM((replicas // 2 * (rows * width // (2 * LANES) + 1), 1, LANES), F32),
                dma, dma, dma,
                dma, dma((chunks,)),
                dma((n - 1, 2)), dma((chunks, n - 1)),
                dma((n, 2)), dma((chunks, n)),
                dma((len(counts),)), dma((len(counts),)),
            ],
            compiler_params=pltpu.CompilerParams(
                collective_id=0, has_side_effects=True, vmem_limit_bytes=52 * 2**20
            ),
        )(
            group_ids,
            gradients.reshape(replicas // 2, 2, rows, cols),
            weights.reshape(replicas, rows, cols),
            master, moment_one, moment_two,
        )
        return new_weights.reshape(rows_all, cols), new_master, new_first, new_second

    return jax.shard_map(
        on_device,
        mesh=mesh,
        in_specs=(P("dp", None, "mp"), P(None, "mp"), P("dp", "mp"), P("dp", "mp"), P("dp", "mp"), P()),
        out_specs=(P(None, "mp"), P("dp", "mp"), P("dp", "mp"), P("dp", "mp")),
        check_vma=False,
    )
```

time: 94.1 us -> 74.5 us (0.79)
  Pallas kernels: 88.3 us -> 68.8 us
    pallas_call x1, Pallas kernels: 88.3 us -> 68.8 us  [on_device(): pl.pallas_call(functools.partial(kernel, n, mp, width, len(counts)), out_...]
where the time goes in v2:
time: 74.5 us; the launch traced here: 74.4 us
  Pallas kernels  68.8 us (92%)
  local copies, waits for them, and re-layouts  4.94 us (7%)
    pallas_call x1, Pallas kernels, on_device(): pl.pallas_call(functools.partial(kernel, n, mp, width, len(counts)), out_...  68.8 us
    unnamed x4, local copies, waits for them, and re-layouts  4.94 us

profile of v2, /device:TPU:1, one launch (start us, length us, event | category | flops | bytes accessed | tf_op | source)
XLA Modules:
  0.0 74.4 jit_solution(7899435156536986394)
XLA Ops:
  0.6 68.8 %shard_map.93 = (bf16[32,16,6144]{2,1,0:T(8,128)(2,1)S(1)}, f32[16,6144]{1,0:T(8,128)S(1)}, f32[16,6144]{1,0:T(8,128)S(1)}, f32[16,6144]{1,0:T(8,128)S(1)}) custom-call(s32[512]{0:T(512)} %ids_ref.1, bf16[16,2,16,6144]{3,2,1,0:T(8,128)(2,1)} %bitcast.4, bf16[32,16,6144]{2,1,0:T(8,128)(2,1)} %bitcast.5, f32[16,6144]{1,0:T(8,128)} %master_hbm.1, ...), custom_call_target="tpu_custom_call" | custom-call | tf_op jit(solution)/shard_map/pallas_call | solution.py:400
  69.4 2.7 %copy.14 = bf16[512,6144]{1,0:T(8,128)(2,1)} copy(bf16[512,6144]{1,0:T(8,128)(2,1)S(1)} %bitcast.3) | data formatting | bytes 12582912
  72.1 0.7 %copy.15 = f32[16,6144]{1,0:T(8,128)} copy(f32[16,6144]{1,0:T(8,128)S(1)} %get-tuple-element.13) | data formatting | bytes 786432
  72.9 0.7 %copy.16 = f32[16,6144]{1,0:T(8,128)} copy(f32[16,6144]{1,0:T(8,128)S(1)} %get-tuple-element.14) | data formatting | bytes 786432
  73.6 0.7 %copy.17 = f32[16,6144]{1,0:T(8,128)} copy(f32[16,6144]{1,0:T(8,128)S(1)} %get-tuple-element.15) | data formatting | bytes 786432

commit v3 on v2

--- a/solution.py
+++ b/solution.py
@@ -19,7 +19,10 @@
 WIDTH = 512
 LANES = 128
 STATIC = 8
-SKEW = 2
+STAGE_DUE = [0.00, 3.47, 6.19, 9.36, 13.72, 17.22, 21.30, 25.04, 29.23, 40.00]
+STAGE_PACE = [2.37, 2.55, 2.91, 2.81, 2.56, 2.76, 2.48, 2.69, 4.82, 4.12]
+TRUST_DUE = [26.48, 30.77, 35.67]
+PUT_DUE = (33.46, 0.22)
 TOP = 32700.0
 TINY = 1e-30
 
@@ -63,36 +66,30 @@
 
 
 def schedule(n, chunks, levels):
-    tasks = []
+    if len(STAGE_DUE) == 2 * n:
+        due, pace, trust, put = STAGE_DUE, STAGE_PACE, TRUST_DUE, PUT_DUE
+    else:
+        due, pace = [2.0 * s for s in range(2 * n)], [1.0] * (2 * n)
+        trust, put = [due[-1]] * (levels + 1), (due[-1], 1.0)
+    after, when = {}, {}
     for k in range(chunks):
-        u = k // 2
         for s in range(2 * n):
-            what = ("R", k, s) if s < n else ("A", k, s - n)
-            tasks.append((u + SKEW * s, 2 * n - s, k, what))
-    tasks.sort()
-    order = [what for *_, what in tasks]
-    last = max(i for i, task in enumerate(order) if task[0] == "R")
-    out, ready, level, since = [], [], 0, 0
-    for i, task in enumerate(order):
+            task = ("R", k, s) if s < n else ("A", k, s - n)
+            after[task] = [last] if s else []
+            when[task] = (due[s] + pace[s] * (k // 2), k)
+            last = task
+        after["P", k, 0] = [last, ("T", 0, levels)]
+        when["P", k, 0] = (put[0] + put[1] * (k // 2), k)
+    for level in range(levels + 1):
+        after["T", 0, level] = [("T", 0, level - 1)] if level else [("R", k, n - 1) for k in range(chunks)]
+        when["T", 0, level] = (trust[min(level, len(trust) - 1)], 0)
+    out, left = [], set(after)
+    while left:
+        free = [task for task in left if not any(other in left for other in after[task])]
+        task = min(free, key=lambda task: (when[task], task))
         out.append(task)
-        if task[0] == "A" and task[2] == n - 1:
-            ready.append(task[1])
-        if i == last:
-            out.append(("T", 0, 0))
-            level, since = 1, 0
-        elif 0 < level <= levels:
-            since += 1
-            if since == 2:
-                out.append(("T", 0, level))
-                level, since = level + 1, 0
-        elif level > levels:
-            for k in ready[:2]:
-                out.append(("P", k, 0))
-            ready = ready[2:]
-    while level <= levels:
-        out.append(("T", 0, level))
-        level += 1
-    return out + [("P", k, 0) for k in ready]
+        left.remove(task)
+    return out
 
 
 def kernel(
@@ -377,6 +374,15 @@
         finish(held_scale.at[:, pl.ds(0, 2**s)], ag_send.at[s, 1])
     for i, slots in enumerate(tiles):
         finish(slots.at[pl.ds(1, len(levels[i]))], t_send.at[i])
+
+
+def put_out(a_ref, b_ref, c_ref, d_ref, a_out, b_out, c_out, d_out, sems):
+    pairs = [(a_ref, a_out), (b_ref, b_out), (c_ref, c_out), (d_ref, d_out)]
+    copies = [pltpu.make_async_copy(src, dst, sems.at[i]) for i, (src, dst) in enumerate(pairs)]
+    for copy in copies:
+        copy.start()
+    for copy in copies:
+        copy.wait()
 
 
 def solution(mesh):
@@ -433,6 +439,17 @@
             weights.reshape(replicas, rows, cols),
             master, moment_one, moment_two,
         )
+        new_weights, new_master, new_first, new_second = pl.pallas_call(
+            put_out,
+            out_shape=(
+                jax.ShapeDtypeStruct((replicas, rows, cols), BF16),
+                *[jax.ShapeDtypeStruct((rows, cols), F32)] * 3,
+            ),
+            in_specs=[vmem] * 4,
+            out_specs=(anywhere,) * 4,
+            scratch_shapes=[dma((4,))],
+            compiler_params=pltpu.CompilerParams(vmem_limit_bytes=2**20),
+        )(new_weights, new_master, new_first, new_second)
         return new_weights.reshape(rows_all, cols), new_master, new_first, new_second
 
     return jax.shard_map(

time: 74.5 us -> 69.2 us (0.929)
  local copies, waits for them, and re-layouts: 4.94 us -> 0 us
    unnamed x4 -> x0, local copies, waits for them, and re-layouts: 4.94 us -> none
    pallas_call x1, Pallas kernels: 68.8 us -> 65.3 us  [on_device(): pl.pallas_call(functools.partial(kernel, n, mp, width, len(counts)), out_...]
    pallas_call x0 -> x1, Pallas kernels: none -> 3.09 us  [on_device(): pl.pallas_call(put_out, out_shape=(jax.ShapeDtypeStruct((replicas, rows,...]
where the time goes in v3:
time: 69.2 us; the launch traced here: 69 us
  Pallas kernels  68.4 us (99%)
    pallas_call x1, Pallas kernels, on_device(): pl.pallas_call(functools.partial(kernel, n, mp, width, len(counts)), out_...  65.3 us
    pallas_call x1, Pallas kernels, on_device(): pl.pallas_call(put_out, out_shape=(jax.ShapeDtypeStruct((replicas, rows,...  3.09 us

profile of v3, /device:TPU:1, one launch (start us, length us, event | category | flops | bytes accessed | tf_op | source)
XLA Modules:
  0.0 69.0 jit_solution(10129212844274609049)
XLA Ops:
  0.6 65.3 %shard_map.93 = (bf16[32,16,6144]{2,1,0:T(8,128)(2,1)S(1)}, f32[16,6144]{1,0:T(8,128)S(1)}, f32[16,6144]{1,0:T(8,128)S(1)}, f32[16,6144]{1,0:T(8,128)S(1)}) custom-call(s32[512]{0:T(512)} %ids_ref.1, bf16[16,2,16,6144]{3,2,1,0:T(8,128)(2,1)} %bitcast.3, bf16[32,16,6144]{2,1,0:T(8,128)(2,1)} %bitcast.4, f32[16,6144]{1,0:T(8,128)} %master_hbm.1, ...), custom_call_target="tpu_custom_call" | custom-call | tf_op jit(solution)/shard_map/pallas_call | solution.py:406
  66.0 3.1 %shard_map.94 = (bf16[32,16,6144]{2,1,0:T(8,128)(2,1)}, f32[16,6144]{1,0:T(8,128)}, f32[16,6144]{1,0:T(8,128)}, f32[16,6144]{1,0:T(8,128)}) custom-call(bf16[32,16,6144]{2,1,0:T(8,128)(2,1)S(1)} %get-tuple-element.12.a_ref, f32[16,6144]{1,0:T(8,128)S(1)} %get-tuple-element.13.b_ref, f32[16,6144]{1,0:T(8,128)S(1)} %get-tuple-element.14.c_ref, ...), custom_call_target="tpu_custom_call" | custom-call | tf_op jit(solution)/shard_map/pallas_call | solution.py:442

commit v4 on v3

--- a/solution.py
+++ b/solution.py
@@ -22,7 +22,7 @@
 STAGE_DUE = [0.00, 3.47, 6.19, 9.36, 13.72, 17.22, 21.30, 25.04, 29.23, 40.00]
 STAGE_PACE = [2.37, 2.55, 2.91, 2.81, 2.56, 2.76, 2.48, 2.69, 4.82, 4.12]
 TRUST_DUE = [26.48, 30.77, 35.67]
-PUT_DUE = (33.46, 0.22)
+PUT_DUE = (37.46, 0.22)
 TOP = 32700.0
 TINY = 1e-30
 
@@ -93,11 +93,11 @@
 
 
 def kernel(
-    n, mp, width, levels_n, ids_ref, grad_ref, w_ref, master_hbm, m1_hbm, m2_hbm,
+    n, mp, width, levels_n, ids_hbm, grad_ref, w_ref, master_hbm, m1_hbm, m2_hbm,
     out_ref, new_master_ref, new_first_ref, new_second_ref,
     mine, raw, temp, peak, kept, codes_out, codes_in, scales_out, scales_in, held, held_scale,
-    update, sums, member, ratio, tiles, state, units,
-    mine_sem, w_sem, own_sem, raw_send, raw_recv, rs_send, rs_recv, ag_send, ag_recv, t_send, t_recv,
+    update, sums, member, ratio, tiles, state, units, ids_ref,
+    mine_sem, w_sem, own_sem, ids_sem, raw_send, raw_recv, rs_send, rs_recv, ag_send, ag_recv, t_send, t_recv,
 ):
     me = lax.axis_index("dp")
     bits = [(me // 2**i) % 2 for i in range(n)]
@@ -135,13 +135,15 @@
         pltpu.make_async_copy(grad_ref.at[:, bits[0], :, span(k)], mine.at[k], mine_sem)
         for k in range(chunks)
     ]
-    for copy in mine_copies:
-        copy.start()
 
     barrier = pltpu.get_barrier_semaphore()
     greeted = [target for level in levels for target in level]
     for target in greeted:
         pl.semaphore_signal(barrier, inc=1, device_id=target, device_id_type=MESH)
+    ids_copy = pltpu.make_async_copy(ids_hbm, ids_ref, ids_sem)
+    ids_copy.start()
+    for copy in mine_copies:
+        copy.start()
     pl.semaphore_wait(barrier, len(greeted))
 
     def finish(ref, sem):
@@ -167,6 +169,7 @@
         copy.start()
     w_copy.start()
 
+    ids_copy.wait()
     lane = lax.broadcasted_iota(I32, (1, LANES), 1)
 
     @pl.loop(0, replicas * rows, unroll=8)
@@ -283,7 +286,9 @@
         first = count if s and piece else 0
         here, there = pl.ds(first, count), pl.ds(first + 2**s, count)
         send(held.at[k, here], held.at[k, there], ag_send.at[s, 0], ag_recv.at[k, s], target)
-        send(held_scale.at[k, here], held_scale.at[k, there], ag_send.at[s, 1], ag_recv.at[k, s], target)
+        if piece:
+            here, there = pl.ds(0, 2**s), pl.ds(2**s, 2**s)
+            send(held_scale.at[k, here], held_scale.at[k, there], ag_send.at[s, 1], ag_recv.at[k, s], target)
 
     def pass_on(k, s):
         if s + 1 < n:
@@ -406,7 +411,7 @@
         new_weights, new_master, new_first, new_second = pl.pallas_call(
             functools.partial(kernel, n, mp, width, len(counts)),
             out_shape=(pltpu.VMEM((replicas, rows, cols), BF16), own, own, own),
-            in_specs=[pl.BlockSpec(memory_space=pltpu.SMEM)] + [anywhere] * 5,
+            in_specs=[anywhere] * 6,
             out_specs=(vmem, vmem, vmem, vmem),
             scratch_shapes=[
                 pltpu.VMEM((chunks, replicas // 2, rows, width), BF16),
@@ -424,7 +429,8 @@
                 [pltpu.VMEM((c, 8, LANES), F32) for c in counts],
                 pltpu.VMEM((3, rows, cols), F32),
                 pltpu.VMEM((replicas // 2 * (rows * width // (2 * LANES) + 1), 1, LANES), F32),
-                dma, dma, dma,
+                pltpu.SMEM((rows_all,), I32),
+                dma, dma, dma, dma,
                 dma, dma((chunks,)),
                 dma((n - 1, 2)), dma((chunks, n - 1)),
                 dma((n, 2)), dma((chunks, n)),

time: 69.2 us -> 68.5 us (0.990)
  Pallas kernels: 68.4 us -> 67.7 us
    pallas_call x1, Pallas kernels: 65.3 us -> 64.6 us  [on_device(): pl.pallas_call(functools.partial(kernel, n, mp, width, len(counts)), out_...]
where the time goes in v4:
time: 68.5 us; the launch traced here: 68.3 us
  Pallas kernels  67.7 us (99%)
    pallas_call x1, Pallas kernels, on_device(): pl.pallas_call(functools.partial(kernel, n, mp, width, len(counts)), out_...  64.6 us
    pallas_call x1, Pallas kernels, on_device(): pl.pallas_call(put_out, out_shape=(jax.ShapeDtypeStruct((replicas, rows,...  3.09 us

profile of v4, /device:TPU:1, one launch (start us, length us, event | category | flops | bytes accessed | tf_op | source)
XLA Modules:
  0.0 68.3 jit_solution(18024177819572196029)
XLA Ops:
  0.6 64.6 %shard_map.93 = (bf16[32,16,6144]{2,1,0:T(8,128)(2,1)S(1)}, f32[16,6144]{1,0:T(8,128)S(1)}, f32[16,6144]{1,0:T(8,128)S(1)}, f32[16,6144]{1,0:T(8,128)S(1)}) custom-call(s32[512]{0:T(512)} %ids_hbm.1, bf16[16,2,16,6144]{3,2,1,0:T(8,128)(2,1)} %bitcast.3, bf16[32,16,6144]{2,1,0:T(8,128)(2,1)} %bitcast.4, f32[16,6144]{1,0:T(8,128)} %master_hbm.1, ...), custom_call_target="tpu_custom_call" | custom-call | tf_op jit(solution)/shard_map/pallas_call | solution.py:411
  65.2 3.1 %shard_map.94 = (bf16[32,16,6144]{2,1,0:T(8,128)(2,1)}, f32[16,6144]{1,0:T(8,128)}, f32[16,6144]{1,0:T(8,128)}, f32[16,6144]{1,0:T(8,128)}) custom-call(bf16[32,16,6144]{2,1,0:T(8,128)(2,1)S(1)} %get-tuple-element.12.a_ref, f32[16,6144]{1,0:T(8,128)S(1)} %get-tuple-element.13.b_ref, f32[16,6144]{1,0:T(8,128)S(1)} %get-tuple-element.14.c_ref, ...), custom_call_target="tpu_custom_call" | custom-call | tf_op jit(solution)/shard_map/pallas_call | solution.py:448

commit v5 on v4

--- a/solution.py
+++ b/solution.py
@@ -19,6 +19,7 @@
 WIDTH = 512
 LANES = 128
 STATIC = 8
+PARTS = 8
 STAGE_DUE = [0.00, 3.47, 6.19, 9.36, 13.72, 17.22, 21.30, 25.04, 29.23, 40.00]
 STAGE_PACE = [2.37, 2.55, 2.91, 2.81, 2.56, 2.76, 2.48, 2.69, 4.82, 4.12]
 TRUST_DUE = [26.48, 30.77, 35.67]
@@ -382,7 +383,9 @@
 
 
 def put_out(a_ref, b_ref, c_ref, d_ref, a_out, b_out, c_out, d_out, sems):
-    pairs = [(a_ref, a_out), (b_ref, b_out), (c_ref, c_out), (d_ref, d_out)]
+    part = a_ref.shape[0] // PARTS
+    pairs = [(a_ref.at[pl.ds(i * part, part)], a_out.at[pl.ds(i * part, part)]) for i in range(PARTS)]
+    pairs += [(b_ref, b_out), (c_ref, c_out), (d_ref, d_out)]
     copies = [pltpu.make_async_copy(src, dst, sems.at[i]) for i, (src, dst) in enumerate(pairs)]
     for copy in copies:
         copy.start()
@@ -453,7 +456,7 @@
             ),
             in_specs=[vmem] * 4,
             out_specs=(anywhere,) * 4,
-            scratch_shapes=[dma((4,))],
+            scratch_shapes=[dma((PARTS + 3,))],
             compiler_params=pltpu.CompilerParams(vmem_limit_bytes=2**20),
         )(new_weights, new_master, new_first, new_second)
         return new_weights.reshape(rows_all, cols), new_master, new_first, new_second

time: 68.5 us -> 68.5 us (level)
  no operation moved by 1% of the time
where the time goes in v5:
time: 68.5 us; the launch traced here: 68.3 us
  Pallas kernels  67.7 us (99%)
    pallas_call x1, Pallas kernels, on_device(): pl.pallas_call(functools.partial(kernel, n, mp, width, len(counts)), out_...  64.6 us
    pallas_call x1, Pallas kernels, on_device(): pl.pallas_call(put_out, out_shape=(jax.ShapeDtypeStruct((replicas, rows,...  3.11 us

profile of v5, /device:TPU:1, one launch (start us, length us, event | category | flops | bytes accessed | tf_op | source)
XLA Modules:
  0.0 68.3 jit_solution(2867398820625370934)
XLA Ops:
  0.6 64.6 %shard_map.93 = (bf16[32,16,6144]{2,1,0:T(8,128)(2,1)S(1)}, f32[16,6144]{1,0:T(8,128)S(1)}, f32[16,6144]{1,0:T(8,128)S(1)}, f32[16,6144]{1,0:T(8,128)S(1)}) custom-call(s32[512]{0:T(512)} %ids_hbm.1, bf16[16,2,16,6144]{3,2,1,0:T(8,128)(2,1)} %bitcast.3, bf16[32,16,6144]{2,1,0:T(8,128)(2,1)} %bitcast.4, f32[16,6144]{1,0:T(8,128)} %master_hbm.1, ...), custom_call_target="tpu_custom_call" | custom-call | tf_op jit(solution)/shard_map/pallas_call | solution.py:414
  65.2 3.1 %shard_map.94 = (bf16[32,16,6144]{2,1,0:T(8,128)(2,1)}, f32[16,6144]{1,0:T(8,128)}, f32[16,6144]{1,0:T(8,128)}, f32[16,6144]{1,0:T(8,128)}) custom-call(bf16[32,16,6144]{2,1,0:T(8,128)(2,1)S(1)} %get-tuple-element.12.a_ref, f32[16,6144]{1,0:T(8,128)S(1)} %get-tuple-element.13.b_ref, f32[16,6144]{1,0:T(8,128)S(1)} %get-tuple-element.14.c_ref, ...), custom_call_target="tpu_custom_call" | custom-call | tf_op jit(solution)/shard_map/pallas_call | solution.py:451
